TPU v7x, 32 devices: a whole 2x2x4 slice. The times are simulated.
32 devices in a mesh: rows: 2 (over y), hidden: 2 (over x), latents: 8 (over z, core).
Axes of the slice: x: 2, y: 2, z: 4, core: 2. Of those that a mesh axis runs over, the one named last changes fastest.
Arguments:
- inputs: bfloat16 [256, 3584], P('rows', ('hidden', 'latents')), may hold values from -6 to 6
- gate_weight: bfloat16 [3584, 14336], P(None, ('hidden', 'latents')), may hold values from -0.09375 to 0.09375
- up_weight: bfloat16 [3584, 14336], P(None, ('hidden', 'latents')), may hold values from -0.09375 to 0.09375
- down_weight: bfloat16 [14336, 3584], P(('hidden', 'latents')), may hold values from -0.046875 to 0.046875
- encoder: bfloat16 [3584, 65536], P('hidden', ('rows', 'latents')), may hold values from -0.09375 to 0.09375
- decoder: bfloat16 [65536, 3584], P(('rows', 'latents'), 'hidden'), may hold values from -0.09375 to 0.09375
- enc_bias: float32 [65536], P(('rows', 'latents')), may hold values from -3 to 3
- dec_bias: float32 [3584], P('hidden'), may hold values from -3 to 3
- shuffle_order: int32 [256], replicated, may hold values from 0 to 255, each once
Outputs:
- recon_out: bfloat16 [256, 3584], P(('rows', 'latents'), 'hidden')
- grad_enc: bfloat16 [3584, 65536], P('hidden', ('rows', 'latents'))
- grad_dec: bfloat16 [65536, 3584], P(('rows', 'latents'), 'hidden')
Inputs may be any that keep to these rules, and one draw needn't show every extreme that they name: shuffle_order names every token index 0 to 255 exactly once.
All inputs are finite; a program needn't handle non-finite values.
Results may differ from a plain program's by a relative error of at most 0.038.
Values may be sent and summed in bfloat16 or wider, within the bound.
A program may use at most 128 MiB of HBM per device.

v0:
```python
import functools
import math

import jax
import jax.numpy as jnp
from jax import lax
from jax.experimental import pallas as pl
from jax.experimental.pallas import tpu as pltpu
from jax.sharding import PartitionSpec as P


smooth_scale = 0.1
sparsity_weight = 0.5
chunks = 2
halves = 2
MESH = pl.DeviceIdType.MESH


class Places:
    def __init__(self, depths):
        here = lax.axis_index("latents")
        self.depths = depths
        self.core = lax.rem(here, 2)
        self.depth = lax.div(here, 2)

    def ahead(self, step):
        return lax.rem(self.depth + step, self.depths)

    def behind(self, step):
        return lax.rem(self.depth + self.depths - step, self.depths)

    def to_core(self):
        return {"latents": self.depth * 2 + 1 - self.core}

    def to_depth(self, depth):
        return {"latents": depth * 2 + self.core}


def to_pair(axis):
    return {axis: 1 - lax.axis_index(axis)}


def greet(places, axes):
    barrier = pltpu.get_barrier_semaphore()
    targets = [places.to_core()] + [to_pair(axis) for axis in axes]
    targets += [places.to_depth(places.ahead(step)) for step in range(1, places.depths)]
    for target in targets:
        pl.semaphore_signal(barrier, inc=1, device_id=target, device_id_type=MESH)
    pl.semaphore_wait(barrier, len(targets))


def send(source, target, sems, number, device):
    copy = pltpu.make_async_remote_copy(
        src_ref=source,
        dst_ref=target,
        send_sem=sems.at[0, number],
        recv_sem=sems.at[1, number],
        device_id=device,
        device_id_type=MESH,
    )
    copy.start()
    return copy


def spread(places, axis, pieces, sems):
    pair, core, depths = lax.axis_index(axis), places.core, places.depths
    own = pieces.at[pair, places.depth, core]
    along, across, inside = [], [], []
    for step in range(1, depths):
        along.append(
            send(own, own, sems, step - 1, places.to_depth(places.ahead(step)))
        )
    across.append(send(own, own, sems, depths, to_pair(axis)))
    inside.append(send(own, own, sems, 2 * depths, places.to_core()))
    for step in range(1, depths):
        along[step - 1].wait_recv()
        piece = pieces.at[pair, places.behind(step), core]
        across.append(send(piece, piece, sems, depths + step, to_pair(axis)))
        inside.append(send(piece, piece, sems, 2 * depths + step, places.to_core()))
    for step in range(depths):
        across[step].wait_recv()
        piece = pieces.at[1 - pair, places.behind(step), core]
        inside.append(
            send(piece, piece, sems, 3 * depths + step, places.to_core())
        )
    for copy in inside:
        copy.wait_recv()
    for copy in along + across + inside:
        copy.wait_send()


def gather_kernel(axis, depths, x_ref, out_ref, pieces, sems):
    places = Places(depths)
    greet(places, (axis,))
    pieces[lax.axis_index(axis), places.depth, places.core] = x_ref[...]
    spread(places, axis, pieces, sems)
    out_ref[...] = pieces[...]


def exchange_sum(places, axis, mine, other, theirs, from_pair, to_send, from_depth, sems):
    depths = places.depths
    order = list(range(1, depths)) + [0]
    across = []
    for step in order:
        depth = places.ahead(step)
        theirs[depth] = other(depth).astype(theirs.dtype)
        across.append(
            send(theirs.at[depth], from_pair.at[depth], sems, step, to_pair(axis))
        )
    along = []
    for place, step in enumerate(order):
        depth = places.ahead(step)
        across[place].wait_recv()
        total = mine(depth) + from_pair[depth].astype(jnp.float32)
        if step:
            to_send[step - 1] = total.astype(to_send.dtype)
            along.append(
                send(
                    to_send.at[step - 1],
                    from_depth.at[step - 1],
                    sems,
                    depths + step,
                    places.to_depth(depth),
                )
            )
    for step in range(1, depths):
        along[step - 1].wait_recv()
        total = total + from_depth[step - 1].astype(jnp.float32)
    for copy in across + along:
        copy.wait_send()
    return total


def rows_kernel(
    depths, x_ref, out_ref, from_core, theirs, from_pair, to_send, from_depth, pieces, sems, more
):
    places = Places(depths)
    core, side = places.core, lax.axis_index("hidden")
    width = out_ref.shape[-1]
    greet(places, ("hidden", "rows"))
    halves = send(x_ref.at[:, 1 - core], from_core, sems, 2 * depths, places.to_core())
    halves.wait_recv()

    def part(which):
        columns = pl.ds(pl.multiple_of(which * width, 128), width)

        def at(depth):
            own = x_ref[depth, core, :, columns].astype(jnp.float32)
            return own + from_core[depth, :, columns].astype(jnp.float32)

        return at

    total = exchange_sum(
        places, "hidden", part(side), part(1 - side), theirs, from_pair, to_send, from_depth, sems
    )
    pieces[lax.axis_index("rows"), places.depth, core] = total.astype(pieces.dtype)
    halves.wait_send()
    spread(places, "rows", pieces, more)
    out_ref[...] = pieces[...]


def recon_kernel(
    depths,
    scale,
    x_ref,
    target_ref,
    bias_ref,
    err_ref,
    recon_ref,
    from_core,
    theirs,
    from_pair,
    to_send,
    from_depth,
    pieces,
    sems,
    more,
):
    places = Places(depths)
    core, side = places.core, lax.axis_index("rows")
    greet(places, ("rows",))
    halves = send(x_ref.at[:, :, 1 - core], from_core, sems, 2 * depths, places.to_core())
    halves.wait_recv()

    def part(which):
        def at(depth):
            own = x_ref[which, depth, core].astype(jnp.float32)
            return own + from_core[which, depth].astype(jnp.float32)

        return at

    total = exchange_sum(
        places, "rows", part(side), part(1 - side), theirs, from_pair, to_send, from_depth, sems
    )
    recon = total + bias_ref[...]
    recon_ref[...] = recon.astype(recon_ref.dtype)
    err = scale * (recon - target_ref[side, places.depth, core].astype(jnp.float32))
    pieces[side, places.depth, core] = err.astype(pieces.dtype)
    halves.wait_send()
    spread(places, "rows", pieces, more)
    err_ref[...] = pieces[...]


def vmem(count):
    return [pl.BlockSpec(memory_space=pltpu.VMEM)] * count


def params(number):
    return pltpu.CompilerParams(collective_id=number, has_side_effects=True)


def gather_features(x, depths):
    shape = (2, depths, 2) + x.shape
    out = pl.pallas_call(
        functools.partial(gather_kernel, "hidden", depths),
        out_shape=jax.ShapeDtypeStruct(shape, x.dtype),
        in_specs=vmem(1),
        out_specs=vmem(1)[0],
        scratch_shapes=[
            pltpu.VMEM(shape, x.dtype),
            pltpu.SemaphoreType.DMA((2, 4 * depths)),
        ],
        compiler_params=params(0),
        name="gather_features",
    )(x)
    return out.reshape(-1, x.shape[-1])


def reduce_scratch(depths, rows, width, core_shape, dtype):
    piece = (rows, width)
    return [
        pltpu.VMEM(core_shape, dtype),
        pltpu.VMEM((depths,) + piece, dtype),
        pltpu.VMEM((depths,) + piece, dtype),
        pltpu.VMEM((depths - 1,) + piece, dtype),
        pltpu.VMEM((depths - 1,) + piece, dtype),
        pltpu.VMEM((2, depths, 2) + piece, dtype),
        pltpu.SemaphoreType.DMA((2, 2 * depths + 1)),
        pltpu.SemaphoreType.DMA((2, 4 * depths)),
    ]


def sum_rows(x, depths):
    rows, width = x.shape[0] // (2 * depths), x.shape[1] // 2
    out = pl.pallas_call(
        functools.partial(rows_kernel, depths),
        out_shape=jax.ShapeDtypeStruct((2, depths, 2, rows, width), x.dtype),
        in_specs=vmem(1),
        out_specs=vmem(1)[0],
        scratch_shapes=reduce_scratch(
            depths, rows, width, (depths, rows, x.shape[1]), x.dtype
        ),
        compiler_params=params(1),
        name="sum_rows",
    )(x.reshape(depths, 2, rows, x.shape[1]))
    return out.reshape(-1, width)


def sum_recon(x, target, bias, scale, depths, number):
    tokens, width = x.shape
    rows = tokens // (4 * depths)
    shape = (2, depths, 2, rows, width)
    err, recon = pl.pallas_call(
        functools.partial(recon_kernel, depths, scale),
        out_shape=(
            jax.ShapeDtypeStruct(shape, x.dtype),
            jax.ShapeDtypeStruct((rows, width), x.dtype),
        ),
        in_specs=vmem(3),
        out_specs=tuple(vmem(2)),
        scratch_shapes=reduce_scratch(depths, rows, width, (2, depths, rows, width), x.dtype),
        compiler_params=params(number),
    )(x.reshape(shape), target.reshape(shape), bias[None, :])
    return err.reshape(tokens, width), recon


def after(x, *others):
    return lax.optimization_barrier((x,) + others)[0]


def add_pair(x, *others):
    if lax.axis_size("hidden") == 2:
        other = lax.ppermute(x, "hidden", [(0, 1), (1, 0)])
        other = after(other, *others) if others else other
        return x.astype(jnp.float32) + other.astype(jnp.float32)
    return lax.psum(x, "hidden").astype(jnp.float32)


def shards(
    inputs, gate_weight, up_weight, down_weight, encoder, decoder, enc_bias, dec_bias, shuffle_order
):
    rows_n, hidden_n, latents_n = map(lax.axis_size, ("rows", "hidden", "latents"))
    tokens = shuffle_order.shape[0]
    features = gate_weight.shape[0]
    depths = latents_n // 2
    fast = (
        rows_n == 2
        and hidden_n == 2
        and latents_n % 2 == 0
        and tokens % (2 * latents_n * 16) == 0
        and features % 256 == 0
        and inputs.shape[1] % 16 == 0
        and inputs.shape[0] % 128 == 0
    )
    if fast:
        gathered = gather_features(inputs.T, depths).T
    else:
        gathered = lax.all_gather(inputs, ("hidden", "latents"), axis=1, tiled=True)
    gate_act = jnp.dot(gathered, gate_weight, preferred_element_type=jnp.float32)
    up_act = jnp.dot(gathered, up_weight, preferred_element_type=jnp.float32)
    hidden = (jax.nn.gelu(gate_act, approximate=True) * up_act).astype(jnp.bfloat16)
    partial_value = jnp.dot(hidden, down_weight, preferred_element_type=jnp.float32)
    partial_value = partial_value.astype(jnp.bfloat16)
    if fast:
        every_row = sum_rows(partial_value, depths)
    else:
        share = lax.psum_scatter(partial_value, "hidden", scatter_dimension=1, tiled=True)
        width_rows = lax.psum(share, "latents")
        every_row = lax.all_gather(width_rows, "rows", axis=0, tiled=True)
    scale = 1.0 / math.sqrt(tokens)
    order = shuffle_order
    if fast:
        order = order.reshape(rows_n * latents_n, halves, -1).transpose(1, 0, 2).reshape(-1)
    columns = lax.broadcasted_iota(jnp.int32, (tokens, tokens), 1)
    one_hot = (order[:, None] == columns).astype(jnp.bfloat16)
    shuffled = jnp.dot(one_hot, every_row, preferred_element_type=jnp.float32)
    shuffled = shuffled.astype(jnp.bfloat16)

    count = chunks if encoder.shape[1] % (128 * chunks) == 0 else 1
    size = encoder.shape[1] // count
    cuts = [slice(i * size, (i + 1) * size) for i in range(count)]
    parts = halves if fast else 1
    share = tokens // parts
    rows = [shuffled[i * share : (i + 1) * share] for i in range(parts)]
    local = []
    for part in range(parts):
        if part:
            rows[part] = after(rows[part], *local[part - 1])
        local.append(
            [
                jnp.dot(
                    rows[part], encoder[:, cut], preferred_element_type=jnp.float32
                ).astype(jnp.bfloat16)
                for cut in cuts
            ]
        )
    pre_act, latent_act, recon_out, d_err, d_pre = [], [], [], [], []
    for part in range(parts):
        pre, latent = [], []
        recon_local = None
        for i, cut in enumerate(cuts):
            summed = add_pair(local[part][i], *d_err[part - 1 : part])
            pre.append(summed + enc_bias[None, cut])
            latent.append(
                (smooth_scale * jax.nn.softplus(pre[i] / smooth_scale)).astype(jnp.bfloat16)
            )
            term = jnp.dot(latent[i], decoder[cut], preferred_element_type=jnp.float32)
            recon_local = term if recon_local is None else recon_local + term
        pre_act.append(pre)
        latent_act.append(jnp.concatenate(latent, axis=1))
        if fast:
            err, recon_rows = sum_recon(
                recon_local.astype(jnp.bfloat16), rows[part], dec_bias, scale, depths, 2 + part
            )
        else:
            recon = lax.psum(recon_local, ("rows", "latents")) + dec_bias[None, :]
            err = (scale * (recon - rows[part].astype(jnp.float32))).astype(jnp.bfloat16)
            row_count = tokens // (rows_n * latents_n)
            first_row = lax.axis_index(("rows", "latents")) * row_count
            recon_rows = lax.dynamic_slice_in_dim(
                recon.astype(jnp.bfloat16), first_row, row_count, 0
            )
        recon_out.append(recon_rows)
        d_err.append(err)
    for part in range(parts):
        d_pre.append([])
        for i, cut in enumerate(cuts):
            back_local = lax.dot_general(
                d_err[part],
                decoder[cut],
                (((1,), (1,)), ((), ())),
                preferred_element_type=jnp.float32,
            ).astype(jnp.bfloat16)
            d_latent = add_pair(back_local)
            gate = jax.nn.sigmoid(pre_act[part][i] / smooth_scale)
            d_pre[part].append(
                ((d_latent + sparsity_weight * scale) * gate).astype(jnp.bfloat16)
            )
    grad_dec = lax.dot_general(
        jnp.concatenate(latent_act, axis=0),
        jnp.concatenate(d_err, axis=0),
        (((0,), (0,)), ((), ())),
        preferred_element_type=jnp.float32,
    ).astype(jnp.bfloat16)
    grad_enc = lax.dot_general(
        shuffled,
        jnp.concatenate([jnp.concatenate(part, axis=1) for part in d_pre], axis=0),
        (((0,), (0,)), ((), ())),
        preferred_element_type=jnp.float32,
    ).astype(jnp.bfloat16)
    return (jnp.concatenate(recon_out, axis=0), grad_enc, grad_dec)


def solution(mesh):
    return jax.shard_map(
        shards,
        mesh=mesh,
        in_specs=(
            P("rows", ("hidden", "latents")),
            P(None, ("hidden", "latents")),
            P(None, ("hidden", "latents")),
            P(("hidden", "latents"), None),
            P("hidden", ("rows", "latents")),
            P(("rows", "latents"), "hidden"),
            P(("rows", "latents")),
            P("hidden"),
            P(),
        ),
        out_specs=(
            P(("rows", "latents"), "hidden"),
            P("hidden", ("rows", "latents")),
            P(("rows", "latents"), "hidden"),
        ),
        check_vma=False,
    )
```

profile of v0, /device:TPU:0, one launch (start us, length us, event | category | flops | bytes accessed | tf_op | source)
XLA Modules:
  0.0 240.3 jit_solution(5089869779980301509)
XLA Ops:
  0.6 0.8 reshape.39
  1.4 0.1 eq.10
  1.5 17.5 %gather_features.1 = bf16[2,4,2,224,128]{4,3,2,1,0:T(8,128)(2,1)} custom-call(bf16[224,128]{1,0:T(8,128)(2,1)} %bitcast.37), custom_call_target="tpu_custom_call" | custom-call | tf_op jit(solution)/shard_map/gather_features/pallas_call | solution.py:214
  19.0 0.0 copy-start
  19.0 4.3 %fusion.109 = f32[128,896]{1,0:T(8,128)S(1)} fusion(bf16[3584,128]{1,0:T(8,128)(2,1)} %bitcast.28, bf16[3584,896]{1,0:T(8,128)(2,1)} %param.10), kind=kOutput, calls=%fused_computation.104 | convolution fusion | flops 822083584 | bytes 7798784 | tf_op jit(solution)/shard_map/dot_general | solution.py:309
  23.4 0.0 copy-done
  23.4 7.8 %convolution_convert_fusion.2 = bf16[128,3584]{1,0:T(8,128)(2,1)} fusion(bf16[896,3584]{1,0:T(8,128)(2,1)} %param.12, bf16[3584,128]{1,0:T(8,128)(2,1)S(1)} %bitcast.29, bf16[3584,896]{1,0:T(8,128)(2,1)} %param.11, f32[128,896]{1,0:T(8,128)S(1)} %fusion.109), kind=kOutput, calls=%fused_computation.10 | convolution fusion | flops 1645772800 | bytes 15138816 | tf_op jit(solution)/shard_map/dot_general | solution.py:312
  31.2 27.7 %sum_rows.1 = bf16[2,4,2,16,1792]{4,3,2,1,0:T(8,128)(2,1)} custom-call(bf16[4,2,16,3584]{3,2,1,0:T(8,128)(2,1)} %bitcast.31), custom_call_target="tpu_custom_call" | custom-call | tf_op jit(solution)/shard_map/sum_rows/pallas_call | solution.py:245
  58.9 1.6 convolution_convert_fusion.3
  60.5 0.0 slice-start
  60.5 0.0 slice-start.1
  60.6 4.4 %fusion.48 = bf16[128,2048]{1,0:T(8,128)(2,1)S(1)} fusion(bf16[1792,4096]{1,0:T(8,128)(2,1)} %param.13, bf16[256,1792]{1,0:T(8,128)(2,1)S(1)} %convolution_convert_fusion.3), kind=kOutput, calls=%fused_computation.40 | convolution fusion | flops 939786240 | bytes 8323072 | tf_op jit(solution)/shard_map/dot_general | solution.py:341
  64.9 0.0 slice-start.2
  64.9 1.6 collective-permute-start
  66.5 4.4 %fusion.54 = bf16[128,2048]{1,0:T(8,128)(2,1)S(1)} fusion(bf16[1792,4096]{1,0:T(8,128)(2,1)} %param.13, bf16[256,1792]{1,0:T(8,128)(2,1)S(1)} %convolution_convert_fusion.3), kind=kOutput, calls=%fused_computation.42 | convolution fusion | flops 939786240 | bytes 8323072 | tf_op jit(solution)/shard_map/dot_general | solution.py:341
  70.9 0.8 collective-permute-start.1
  71.7 0.8 fusion.107
  72.5 5.2 %fusion.51 = bf16[128,2048]{1,0:T(8,128)(2,1)} fusion(bf16[128,1792]{1,0:T(8,128)(2,1)S(1)} %get-tuple-element.11, bf16[1792,4096]{1,0:T(8,128)(2,1)} %param.13), kind=kOutput, calls=%fused_computation.41 | convolution fusion | flops 939786240 | bytes 8323072 | tf_op jit(solution)/shard_map/dot_general | solution.py:341
  77.8 1.2 collective-permute-start.2
  79.0 0.0 copy-done.2
  79.0 0.0 slice-done
  79.0 0.0 slice-done.1
  79.0 0.0 slice-done.3
  79.0 1.2 fusion.57
  80.3 0.8 collective-permute-start.3
  81.1 0.6 broadcast_in_dim.2.bias_ref
  81.8 9.3 %collective-permute-done.1 = bf16[128,2048]{1,0:T(8,128)(2,1)S(1)} collective-permute-done((bf16[128,2048]{1,0:T(8,128)(2,1)S(1)}, bf16[128,2048]{1,0:T(8,128)(2,1)S(1)}, u32[]{:S(2)}, u32[]{:S(2)}) %collective-permute-start.1) | collective-permute-done | bytes 524320 | tf_op jit(solution)/shard_map/ppermute | solution.py:283
  91.0 0.8 fusion.78
  91.9 1.2 fusion.14
  93.1 0.0 collective-permute-done
  93.1 0.8 copy-done.1
  93.9 0.8 fusion.76
  94.7 0.0 copy-start.4
  94.7 0.8 copy-done.4
  95.5 1.9 fusion.33
  97.4 22.0 %shard_map.112 = (bf16[2,4,2,8,1792]{4,3,2,1,0:T(8,128)(2,1)}, bf16[8,1792]{1,0:T(8,128)(2,1)}) custom-call(bf16[2,4,2,8,1792]{4,3,2,1,0:T(8,128)(2,1)} %bitcast.34, bf16[2,4,2,8,1792]{4,3,2,1,0:T(8,128)(2,1)} %bitcast.33, f32[1,1792]{1,0:T(1,128)} %broadcast_in_dim.2.bias_ref), custom_call_target="tpu_custom_call" | custom-call | tf_op jit(solution)/shard_map/pallas_call | solution.py:263
  119.5 0.0 slice-start.8
  119.5 0.0 slice-start.9
  119.5 6.7 %fusion.42 = bf16[128,2048]{1,0:T(8,128)(2,1)} fusion(bf16[128,1792]{1,0:T(8,128)(2,1)} %bitcast.44, bf16[4096,1792]{1,0:T(8,128)(2,1)} %param.14), kind=kOutput, calls=%fused_computation.38 | convolution fusion | flops 939786240 | bytes 8323072 | tf_op jit(solution)/shard_map/dot_general | solution.py:378
  126.2 6.5 %fusion.36 = bf16[128,2048]{1,0:T(8,128)(2,1)} fusion(bf16[128,1792]{1,0:T(8,128)(2,1)S(1)} %bitcast.46, bf16[4096,1792]{1,0:T(8,128)(2,1)} %param.14), kind=kOutput, calls=%fused_computation.36 | convolution fusion | flops 939786240 | bytes 8323072 | tf_op jit(solution)/shard_map/dot_general | solution.py:378
  132.7 0.0 collective-permute-done.2
  132.7 2.0 fusion.80
  134.7 0.0 collective-permute-done.3
  134.7 0.8 fusion.82
  135.5 0.8 copy-done.6
  136.3 4.4 %fusion.12 = f32[128,1792]{1,0:T(8,128)S(1)} fusion(bf16[128,2048]{1,0:T(8,128)(2,1)S(1)} %fusion.82, bf16[4096,1792]{1,0:T(8,128)(2,1)} %param.14), kind=kOutput, calls=%fused_computation.15 | convolution fusion | flops 939524096 | bytes 8781824 | tf_op jit(solution)/shard_map/dot_general | solution.py:357
  140.7 2.0 fusion.30
  142.7 21.9 %shard_map.113 = (bf16[2,4,2,8,1792]{4,3,2,1,0:T(8,128)(2,1)}, bf16[8,1792]{1,0:T(8,128)(2,1)}) custom-call(bf16[2,4,2,8,1792]{4,3,2,1,0:T(8,128)(2,1)} %bitcast.35, bf16[2,4,2,8,1792]{4,3,2,1,0:T(8,128)(2,1)} %bitcast.32, f32[1,1792]{1,0:T(1,128)} %broadcast_in_dim.2.bias_ref), custom_call_target="tpu_custom_call" | custom-call | tf_op jit(solution)/shard_map/pallas_call | solution.py:263
  164.6 0.0 copy-start.12
  164.6 6.6 %fusion.45 = bf16[128,2048]{1,0:T(8,128)(2,1)} fusion(bf16[128,1792]{1,0:T(8,128)(2,1)} %bitcast.47, bf16[4096,1792]{1,0:T(8,128)(2,1)} %param.14), kind=kOutput, calls=%fused_computation.39 | convolution fusion | flops 939786240 | bytes 8323072 | tf_op jit(solution)/shard_map/dot_general | solution.py:378
  171.1 6.4 %fusion.39 = bf16[128,2048]{1,0:T(8,128)(2,1)} fusion(bf16[128,1792]{1,0:T(8,128)(2,1)S(1)} %bitcast.49, bf16[4096,1792]{1,0:T(8,128)(2,1)} %param.14), kind=kOutput, calls=%fused_computation.37 | convolution fusion | flops 939786240 | bytes 8323072 | tf_op jit(solution)/shard_map/dot_general | solution.py:378
  177.5 1.5 collective-permute-start.4
  179.0 0.6 collective-permute-start.5
  179.6 1.5 collective-permute-start.6
  181.0 0.6 collective-permute-start.7
  181.6 0.6 pad_maximum_fusion
  182.2 11.6 %convolution_convert_fusion = bf16[4096,1792]{1,0:T(8,128)(2,1)} fusion(bf16[128,2048]{1,0:T(8,128)(2,1)} %copy-done.6, bf16[128,2048]{1,0:T(8,128)(2,1)} %copy-done.5, bf16[128,2048]{1,0:T(8,128)(2,1)} %copy-done.3, bf16[128,2048]{1,0:T(8,128)(2,1)} %copy-done.4, bf16[128,1792]{1,0:T(8,128)(2,1)} %bitcast.48, bf16[128,1792]{1,0:T(8,128)(2,1)} %bitcast.45), kind=kOutput, calls=%fused_computation | convolution fusion | flops 3775660032 | bytes 17694720 | tf_op jit(solution)/shard_map/dot_general | solution.py:389
  193.8 0.0 collective-permute-done.4
  193.8 21.3 %collective-permute-done.6 = bf16[128,2048]{1,0:T(8,128)(2,1)} collective-permute-done((bf16[128,2048]{1,0:T(8,128)(2,1)}, bf16[128,2048]{1,0:T(8,128)(2,1)}, u32[]{:S(2)}, u32[]{:S(2)}) %collective-permute-start.6) | collective-permute-done | bytes 524320 | tf_op jit(solution)/shard_map/ppermute | solution.py:283
  215.1 3.0 %multiply_convert_fusion.3 = (bf16[128,2048]{1,0:T(8,128)(2,1)S(1)}, bf16[128,2048]{1,0:T(8,128)(2,1)S(1)}) fusion(bf16[128,2048]{1,0:T(8,128)(2,1)} %collective-permute-done.4, bf16[128,2048]{1,0:T(8,128)(2,1)} %fusion.36, bf16[128,2048]{1,0:T(8,128)(2,1)} %copy-done.1, bf16[128,2048]{1,0:T(8,128)(2,1)S(1)} %fusion.48, f32[2048]{0:T(1024)S(1)} %get-tuple-element.19, ...), kind=kLoop, calls=%fused_computation.71 | loop fusion | flops 7340032 | bytes 5251072 | tf_op jit(solution)/shard_map/convert_element_type | solution.py:387
  218.1 0.0 collective-permute-done.5
  218.2 7.6 %collective-permute-done.7 = bf16[128,2048]{1,0:T(8,128)(2,1)} collective-permute-done((bf16[128,2048]{1,0:T(8,128)(2,1)}, bf16[128,2048]{1,0:T(8,128)(2,1)}, u32[]{:S(2)}, u32[]{:S(2)}) %collective-permute-start.7) | collective-permute-done | bytes 524320 | tf_op jit(solution)/shard_map/ppermute | solution.py:283
  225.8 2.5 %multiply_convert_fusion.2 = (bf16[128,2048]{1,0:T(8,128)(2,1)S(1)}, bf16[128,2048]{1,0:T(8,128)(2,1)S(1)}) fusion(bf16[128,2048]{1,0:T(8,128)(2,1)} %collective-permute-done.5, bf16[128,2048]{1,0:T(8,128)(2,1)} %fusion.42, bf16[128,2048]{1,0:T(8,128)(2,1)S(1)} %collective-permute-done.1, bf16[128,2048]{1,0:T(8,128)(2,1)S(1)} %fusion.54, ...), kind=kLoop, calls=%fused_computation.70 | loop fusion | flops 7340032 | bytes 5251072 | tf_op jit(solution)/shard_map/convert_element_type | solution.py:387
  228.3 12.0 %convolution_convert_fusion.1 = bf16[1792,4096]{1,0:T(8,128)(2,1)} fusion(bf16[256,1792]{1,0:T(8,128)(2,1)S(1)} %convolution_convert_fusion.3, bf16[128,2048]{1,0:T(8,128)(2,1)S(1)} %get-tuple-element.24, bf16[128,2048]{1,0:T(8,128)(2,1)S(1)} %get-tuple-element.22, bf16[128,2048]{1,0:T(8,128)(2,1)S(1)} %get-tuple-element.23, ...), kind=kOutput, calls=%fused_computation.1 | convolution fusion | flops 3773825024 | bytes 17694720 | tf_op jit(solution)/shard_map/dot_general | solution.py:395
  (39 shorter events, 0.1 us)
Async XLA Ops:
  19.0 4.3 %copy-start = (bf16[2,4,2,224,128]{4,3,2,1,0:T(8,128)(2,1)S(1)}, bf16[2,4,2,224,128]{4,3,2,1,0:T(8,128)(2,1)}, u32[]{:S(2)}) copy-start(bf16[2,4,2,224,128]{4,3,2,1,0:T(8,128)(2,1)} %gather_features.1) | copy-start | bytes 2752516
  60.5 18.5 %slice-start = ((s8[14680064]{0:T(1024)(128)(4,1)}), s8[4194304]{0:T(1024)(128)(4,1)S(1)}, s32[]{:S(2)}) async-start(s8[14680064]{0:T(1024)(128)(4,1)} %bitcast.38), calls=%async_computation | async-start | bytes 8388608
  60.5 18.5 %slice-start.1 = ((s8[14680064]{0:T(1024)(128)(4,1)}), s8[4194304]{0:T(1024)(128)(4,1)S(1)}, s32[]{:S(2)}) async-start(s8[14680064]{0:T(1024)(128)(4,1)} %bitcast.38), calls=%async_computation.1 | async-start | bytes 8388608
  64.9 14.1 %slice-start.2 = ((s8[14680064]{0:T(1024)(128)(4,1)}), s8[4194304]{0:T(1024)(128)(4,1)S(1)}, s32[]{:S(2)}) async-start(s8[14680064]{0:T(1024)(128)(4,1)} %bitcast.38), calls=%async_computation.2 | async-start | bytes 8388608
  64.9 28.1 %collective-permute-start = (bf16[128,2048]{1,0:T(8,128)(2,1)S(1)}, bf16[128,2048]{1,0:T(8,128)(2,1)S(1)}, u32[]{:S(2)}, u32[]{:S(2)}) collective-permute-start(bf16[128,2048]{1,0:T(8,128)(2,1)S(1)} %fusion.48), channel_id=1, source_target_pairs={{0,8},{8,0},{1,9},{9,1},{2,10},{10,2},{3,11},{11,3},{4,12},{12,4},... | collective-permute-start | bytes 1572872 | tf_op jit(solution)/shard_map/ppermute | solution.py:283
  66.5 25.3 %slice-start.4 = ((s8[14680064]{0:T(1024)(128)(4,1)}), s8[4194304]{0:T(1024)(128)(4,1)S(1)}, s32[]{:S(2)}) async-start(s8[14680064]{0:T(1024)(128)(4,1)} %bitcast.40), calls=%async_computation.4 | async-start | bytes 8388608
  66.5 25.3 %slice-start.5 = ((s8[14680064]{0:T(1024)(128)(4,1)}), s8[4194304]{0:T(1024)(128)(4,1)S(1)}, s32[]{:S(2)}) async-start(s8[14680064]{0:T(1024)(128)(4,1)} %bitcast.40), calls=%async_computation.5 | async-start | bytes 8388608
  70.9 20.2 %collective-permute-start.1 = (bf16[128,2048]{1,0:T(8,128)(2,1)S(1)}, bf16[128,2048]{1,0:T(8,128)(2,1)S(1)}, u32[]{:S(2)}, u32[]{:S(2)}) collective-permute-start(bf16[128,2048]{1,0:T(8,128)(2,1)S(1)} %fusion.54), channel_id=1, source_target_pairs={{0,8},{8,0},{1,9},{9,1},{2,10},{10,2},{3,11},{11,3},{4,12},{12,4},... | collective-permute-start | bytes 1572872 | tf_op jit(solution)/shard_map/ppermute | solution.py:283
  72.5 6.5 %copy-start.2 = (bf16[128,1792]{1,0:T(8,128)(2,1)}, bf16[128,1792]{1,0:T(8,128)(2,1)S(1)}, u32[]{:S(2)}) copy-start(bf16[128,1792]{1,0:T(8,128)(2,1)S(1)} %get-tuple-element.11) | copy-start | bytes 1376260
  72.5 6.5 %slice-start.3 = ((s8[14680064]{0:T(1024)(128)(4,1)}), s8[2097152]{0:T(1024)(128)(4,1)S(1)}, s32[]{:S(2)}) async-start(s8[14680064]{0:T(1024)(128)(4,1)} %bitcast.38), calls=%async_computation.3 | async-start | bytes 4194304
  72.5 19.3 %slice-start.6 = ((s8[14680064]{0:T(1024)(128)(4,1)}), s8[4194304]{0:T(1024)(128)(4,1)S(1)}, s32[]{:S(2)}) async-start(s8[14680064]{0:T(1024)(128)(4,1)} %bitcast.40), calls=%async_computation.6 | async-start | bytes 8388608
  77.8 3.4 %copy-start.10 = (f32[1792]{0:T(1024)S(1)}, f32[1792]{0:T(1024)}, u32[]{:S(2)}) copy-start(f32[1792]{0:T(1024)} %param.16) | copy-start | bytes 21508
  77.8 4.0 %copy-start.9 = (f32[4096]{0:T(1024)S(1)}, f32[4096]{0:T(1024)}, u32[]{:S(2)}) copy-start(f32[4096]{0:T(1024)} %param.15) | copy-start | bytes 49156
  77.8 14.1 %slice-start.7 = ((s8[14680064]{0:T(1024)(128)(4,1)}), s8[2097152]{0:T(1024)(128)(4,1)S(1)}, s32[]{:S(2)}) async-start(s8[14680064]{0:T(1024)(128)(4,1)} %bitcast.40), calls=%async_computation.7 | async-start | bytes 4194304
  77.8 54.9 %collective-permute-start.2 = (bf16[128,2048]{1,0:T(8,128)(2,1)}, bf16[128,2048]{1,0:T(8,128)(2,1)}, u32[]{:S(2)}, u32[]{:S(2)}) collective-permute-start(bf16[128,2048]{1,0:T(8,128)(2,1)} %fusion.51), channel_id=1, source_target_pairs={{0,8},{8,0},{1,9},{9,1},{2,10},{10,2},{3,11},{11,3},{4,12},{12,4},... | collective-permute-start | bytes 1572872 | tf_op jit(solution)/shard_map/ppermute | solution.py:283
  80.3 54.4 %collective-permute-start.3 = (bf16[128,2048]{1,0:T(8,128)(2,1)S(1)}, bf16[128,2048]{1,0:T(8,128)(2,1)S(1)}, u32[]{:S(2)}, u32[]{:S(2)}) collective-permute-start(bf16[128,2048]{1,0:T(8,128)(2,1)S(1)} %fusion.57), channel_id=1, source_target_pairs={{0,8},{8,0},{1,9},{9,1},{2,10},{10,2},{3,11},{11,3},{4,12},{12,4},... | collective-permute-start | bytes 1572872 | tf_op jit(solution)/shard_map/ppermute | solution.py:283
  91.9 1.2 copy-start.3
  93.1 0.8 copy-start.1
  94.7 0.8 copy-start.4
  119.5 6.7 %copy-start.11 = (bf16[2,4,2,8,1792]{4,3,2,1,0:T(8,128)(2,1)S(1)}, bf16[2,4,2,8,1792]{4,3,2,1,0:T(8,128)(2,1)}, u32[]{:S(2)}) copy-start(bf16[2,4,2,8,1792]{4,3,2,1,0:T(8,128)(2,1)} %get-tuple-element.12) | copy-start | bytes 1376260
  119.5 21.2 %slice-start.8 = ((s8[14680064]{0:T(1024)(128)(4,1)}), s8[2097152]{0:T(1024)(128)(4,1)S(1)}, s32[]{:S(2)}) async-start(s8[14680064]{0:T(1024)(128)(4,1)} %bitcast.42), calls=%async_computation.8 | async-start | bytes 4194304
  119.5 21.2 %slice-start.9 = ((s8[14680064]{0:T(1024)(128)(4,1)}), s8[4194304]{0:T(1024)(128)(4,1)S(1)}, s32[]{:S(2)}) async-start(s8[14680064]{0:T(1024)(128)(4,1)} %bitcast.42), calls=%async_computation.9 | async-start | bytes 8388608
  126.2 14.5 %slice-start.10 = ((s8[14680064]{0:T(1024)(128)(4,1)}), s8[4194304]{0:T(1024)(128)(4,1)S(1)}, s32[]{:S(2)}) async-start(s8[14680064]{0:T(1024)(128)(4,1)} %bitcast.42), calls=%async_computation.10 | async-start | bytes 8388608
  134.7 8.0 %copy-start.5 = (bf16[128,2048]{1,0:T(8,128)(2,1)}, bf16[128,2048]{1,0:T(8,128)(2,1)S(1)}, u32[]{:S(2)}) copy-start(bf16[128,2048]{1,0:T(8,128)(2,1)S(1)} %fusion.80) | copy-start | bytes 1572868
  135.5 0.8 copy-start.6
  136.3 4.4 %slice-start.11 = ((s8[14680064]{0:T(1024)(128)(4,1)}), s8[4194304]{0:T(1024)(128)(4,1)S(1)}, s32[]{:S(2)}) async-start(s8[14680064]{0:T(1024)(128)(4,1)} %bitcast.42), calls=%async_computation.11 | async-start | bytes 8388608
  164.6 6.6 %copy-start.12 = (bf16[2,4,2,8,1792]{4,3,2,1,0:T(8,128)(2,1)S(1)}, bf16[2,4,2,8,1792]{4,3,2,1,0:T(8,128)(2,1)}, u32[]{:S(2)}) copy-start(bf16[2,4,2,8,1792]{4,3,2,1,0:T(8,128)(2,1)} %get-tuple-element.16) | copy-start | bytes 1376260
  171.1 10.4 %copy-start.7 = (bf16[8,1792]{1,0:T(8,128)(2,1)S(1)}, bf16[8,1792]{1,0:T(8,128)(2,1)}, u32[]{:S(2)}) copy-start(bf16[8,1792]{1,0:T(8,128)(2,1)} %get-tuple-element.10) | copy-start | bytes 86020
  171.1 10.4 %copy-start.8 = (bf16[8,1792]{1,0:T(8,128)(2,1)S(1)}, bf16[8,1792]{1,0:T(8,128)(2,1)}, u32[]{:S(2)}) copy-start(bf16[8,1792]{1,0:T(8,128)(2,1)} %get-tuple-element.15) | copy-start | bytes 86020
  177.5 16.2 %collective-permute-start.4 = (bf16[128,2048]{1,0:T(8,128)(2,1)}, bf16[128,2048]{1,0:T(8,128)(2,1)}, u32[]{:S(2)}, u32[]{:S(2)}) collective-permute-start(bf16[128,2048]{1,0:T(8,128)(2,1)} %fusion.36), channel_id=1, source_target_pairs={{0,8},{8,0},{1,9},{9,1},{2,10},{10,2},{3,11},{11,3},{4,12},{12,4},... | collective-permute-start | bytes 1572872 | tf_op jit(solution)/shard_map/ppermute | solution.py:283
  179.0 39.2 %collective-permute-start.5 = (bf16[128,2048]{1,0:T(8,128)(2,1)}, bf16[128,2048]{1,0:T(8,128)(2,1)}, u32[]{:S(2)}, u32[]{:S(2)}) collective-permute-start(bf16[128,2048]{1,0:T(8,128)(2,1)} %fusion.42), channel_id=1, source_target_pairs={{0,8},{8,0},{1,9},{9,1},{2,10},{10,2},{3,11},{11,3},{4,12},{12,4},... | collective-permute-start | bytes 1572872 | tf_op jit(solution)/shard_map/ppermute | solution.py:283
  179.6 35.6 %collective-permute-start.6 = (bf16[128,2048]{1,0:T(8,128)(2,1)}, bf16[128,2048]{1,0:T(8,128)(2,1)}, u32[]{:S(2)}, u32[]{:S(2)}) collective-permute-start(bf16[128,2048]{1,0:T(8,128)(2,1)} %fusion.39), channel_id=1, source_target_pairs={{0,8},{8,0},{1,9},{9,1},{2,10},{10,2},{3,11},{11,3},{4,12},{12,4},... | collective-permute-start | bytes 1572872 | tf_op jit(solution)/shard_map/ppermute | solution.py:283
  181.0 44.7 %collective-permute-start.7 = (bf16[128,2048]{1,0:T(8,128)(2,1)}, bf16[128,2048]{1,0:T(8,128)(2,1)}, u32[]{:S(2)}, u32[]{:S(2)}) collective-permute-start(bf16[128,2048]{1,0:T(8,128)(2,1)} %fusion.45), channel_id=1, source_target_pairs={{0,8},{8,0},{1,9},{9,1},{2,10},{10,2},{3,11},{11,3},{4,12},{12,4},... | collective-permute-start | bytes 1572872 | tf_op jit(solution)/shard_map/ppermute | solution.py:283
where the time goes:
time: 241 us; the launch traced here: 240 us
  Pallas kernels  89.1 us (37%)
  matrix products  88.1 us (37%)
  waiting for transfers between devices  38.2 us (16%)
  other arithmetic  10.5 us (4%)
  starting transfers between devices  8.55 us (4%)
  local copies, waits for them, and re-layouts  4.78 us (2%)
    pallas_call x2, Pallas kernels, sum_recon(): pl.pallas_call(functools.partial(recon_kernel, depths, scale), out_shape=...  43.9 us
    ppermute x8, waiting for transfers between devices, add_pair(): other = lax.ppermute(x, 'hidden', [(0, 1), (1, 0)])  38.2 us
    pallas_call x1, Pallas kernels, sum_rows(): pl.pallas_call(functools.partial(rows_kernel, depths), out_shape=jax.Shap...  27.7 us
    dot_general x4, matrix products, shards(): lax.dot_general(d_err[part], decoder[cut], (((1,), (1,)), ((), ())), pref...  26.1 us
    pallas_call x1, Pallas kernels, gather_features(): pl.pallas_call(functools.partial(gather_kernel, 'hidden', depths), out_sh...  17.5 us
    dot_general x4, matrix products, shards(): jnp.dot(rows[part], encoder[:, cut], preferred_element_type=jnp.float32)  15.2 us
    dot_general x1, matrix products, shards(): lax.dot_general(shuffled, jnp.concatenate([jnp.concatenate(part, axis=1)...  12 us
    dot_general x1, matrix products, shards(): lax.dot_general(jnp.concatenate(latent_act, axis=0), jnp.concatenate(d_er...  11.6 us
  transfers between devices with their start and end apart: 8, of which 3 were waited for; matrix products, arithmetic and copies ran while one was open for 20% of the time, Pallas kernels for 9%

commit v1 on v0

--- a/solution.py
+++ b/solution.py
@@ -13,6 +13,7 @@
 sparsity_weight = 0.5
 chunks = 2
 halves = 2
+turn_kernels = True
 MESH = pl.DeviceIdType.MESH
 
 
@@ -272,6 +273,83 @@
         compiler_params=params(number),
     )(x.reshape(shape), target.reshape(shape), bias[None, :])
     return err.reshape(tokens, width), recon
+
+
+def turn_kernel(err_ref, decoder_ref, out_ref):
+    out_ref[...] = lax.dot_general(
+        err_ref[...],
+        decoder_ref[...],
+        (((1,), (1,)), ((), ())),
+        preferred_element_type=jnp.float32,
+    ).astype(out_ref.dtype)
+
+
+def turn(err, decoder, which, count):
+    size = decoder.shape[0] // count
+    block = 512 if size % 512 == 0 else size
+    steps = size // block
+    return pl.pallas_call(
+        turn_kernel,
+        grid=(steps,),
+        out_shape=jax.ShapeDtypeStruct((err.shape[0], size), err.dtype),
+        in_specs=[
+            pl.BlockSpec(err.shape, lambda i: (0, 0)),
+            pl.BlockSpec((block, decoder.shape[1]), lambda i: (which * steps + i, 0)),
+        ],
+        out_specs=pl.BlockSpec((err.shape[0], block), lambda i: (0, i)),
+        cost_estimate=pl.CostEstimate(
+            flops=2 * err.size * size,
+            bytes_accessed=2 * (err.size + size * decoder.shape[1] + err.shape[0] * size),
+            transcendentals=0,
+        ),
+        name="turn",
+    )(err, decoder)
+
+
+def weight_kernel(count, left_ref, *refs):
+    rights, out_ref, right = refs[:count], refs[-2], refs[-1]
+
+    @pl.when(pl.program_id(0) == 0)
+    def _():
+        at = 0
+        for ref in rights:
+            right[at : at + ref.shape[0]] = ref[...]
+            at += ref.shape[0]
+
+    out_ref[...] = lax.dot_general(
+        left_ref[...],
+        right[...],
+        (((0,), (0,)), ((), ())),
+        preferred_element_type=jnp.float32,
+    ).astype(out_ref.dtype)
+
+
+def weight_columns(left, rights, which, count, into):
+    tokens, features = left.shape
+    size = rights[0].shape[1]
+    block = 256 if features % 256 == 0 else features
+    whole = pl.BlockSpec(rights[0].shape, lambda i: (0, 0))
+    specs = [pl.BlockSpec((tokens, block), lambda i: (0, i))] + [whole] * len(rights)
+    args = [left] + rights
+    aliases = {}
+    if into is not None:
+        aliases = {len(args): 0}
+        specs.append(pl.BlockSpec(memory_space=pl.ANY))
+        args.append(into)
+    return pl.pallas_call(
+        functools.partial(weight_kernel, len(rights)),
+        grid=(features // block,),
+        out_shape=jax.ShapeDtypeStruct((features, size * count), left.dtype),
+        in_specs=specs,
+        out_specs=pl.BlockSpec((block, size), lambda i: (i, which)),
+        scratch_shapes=[pltpu.VMEM((tokens, size), left.dtype)],
+        input_output_aliases=aliases,
+        cost_estimate=pl.CostEstimate(
+            flops=2 * left.size * size,
+            bytes_accessed=2 * (left.size + tokens * size + features * size),
+            transcendentals=0,
+        ),
+    )(*args)
 
 
 def after(x, *others):
@@ -375,12 +453,15 @@
     for part in range(parts):
         d_pre.append([])
         for i, cut in enumerate(cuts):
-            back_local = lax.dot_general(
-                d_err[part],
-                decoder[cut],
-                (((1,), (1,)), ((), ())),
-                preferred_element_type=jnp.float32,
-            ).astype(jnp.bfloat16)
+            if fast and turn_kernels:
+                back_local = turn(d_err[part], decoder, i, count)
+            else:
+                back_local = lax.dot_general(
+                    d_err[part],
+                    decoder[cut],
+                    (((1,), (1,)), ((), ())),
+                    preferred_element_type=jnp.float32,
+                ).astype(jnp.bfloat16)
             d_latent = add_pair(back_local)
             gate = jax.nn.sigmoid(pre_act[part][i] / smooth_scale)
             d_pre[part].append(
@@ -392,12 +473,19 @@
         (((0,), (0,)), ((), ())),
         preferred_element_type=jnp.float32,
     ).astype(jnp.bfloat16)
-    grad_enc = lax.dot_general(
-        shuffled,
-        jnp.concatenate([jnp.concatenate(part, axis=1) for part in d_pre], axis=0),
-        (((0,), (0,)), ((), ())),
-        preferred_element_type=jnp.float32,
-    ).astype(jnp.bfloat16)
+    if fast:
+        grad_enc = None
+        for i in range(count):
+            grad_enc = weight_columns(
+                shuffled, [part[i] for part in d_pre], i, count, grad_enc
+            )
+    else:
+        grad_enc = lax.dot_general(
+            shuffled,
+            jnp.concatenate([jnp.concatenate(part, axis=1) for part in d_pre], axis=0),
+            (((0,), (0,)), ((), ())),
+            preferred_element_type=jnp.float32,
+        ).astype(jnp.bfloat16)
     return (jnp.concatenate(recon_out, axis=0), grad_enc, grad_dec)
 
 

time: 241 us -> 247 us (1.025)
  Pallas kernels: 89.1 us -> 129 us
  matrix products: 88.1 us -> 55.8 us
    pallas_call x0 -> x6, Pallas kernels: none -> 39.8 us  [the longest x4 24.6 us: turn(): pl.pallas_call(turn_kernel, grid=(steps,), out_shape=jax.ShapeDtypeStruct...]
    dot_general x5 -> x0, matrix products: 38.1 us -> none  [the longest x4 26.1 us: shards(): lax.dot_general(d_err[part], decoder[cut], (((1,), (1,)), ((), ())), pref...]
    dot_general x4, matrix products: 15.2 us -> 18.3 us  [shards(): jnp.dot(rows[part], encoder[:, cut], preferred_element_type=jnp.float32)]
    dot_general x4, matrix products: 9.44 us -> 12.4 us  [shards(): term = jnp.dot(latent[i], decoder[cut], preferred_element_type=jnp.float32)]
  transfers between devices with their start and end apart: 8 -> 8, of which waited for: 3 -> 3; matrix products, arithmetic and copies ran while one was open for 20% -> 17% of each run, Pallas kernels for 9% -> 15%
where the time goes in v1:
time: 247 us; the launch traced here: 246 us
  Pallas kernels  129 us (52%)
  matrix products  55.8 us (23%)
  waiting for transfers between devices  36.8 us (15%)
  other arithmetic  12 us (5%)
  starting transfers between devices  8.33 us (3%)
  local copies, waits for them, and re-layouts  3.27 us (1%)
    pallas_call x2, Pallas kernels, sum_recon(): pl.pallas_call(functools.partial(recon_kernel, depths, scale), out_shape=...  44 us
    ppermute x8, waiting for transfers between devices, add_pair(): other = lax.ppermute(x, 'hidden', [(0, 1), (1, 0)])  36.8 us
    pallas_call x1, Pallas kernels, sum_rows(): pl.pallas_call(functools.partial(rows_kernel, depths), out_shape=jax.Shap...  27.6 us
    pallas_call x4, Pallas kernels, turn(): pl.pallas_call(turn_kernel, grid=(steps,), out_shape=jax.ShapeDtypeStruct...  24.6 us
    dot_general x4, matrix products, shards(): jnp.dot(rows[part], encoder[:, cut], preferred_element_type=jnp.float32)  18.3 us
    pallas_call x1, Pallas kernels, gather_features(): pl.pallas_call(functools.partial(gather_kernel, 'hidden', depths), out_sh...  17.5 us
    pallas_call x2, Pallas kernels, weight_columns(): pl.pallas_call(functools.partial(weight_kernel, len(rights)), grid=(featu...  15.2 us
    dot_general x4, matrix products, shards(): term = jnp.dot(latent[i], decoder[cut], preferred_element_type=jnp.float32)  12.4 us
  transfers between devices with their start and end apart: 8, of which 3 were waited for; matrix products, arithmetic and copies ran while one was open for 17% of the time, Pallas kernels for 15%

profile of v1, /device:TPU:0, one launch (start us, length us, event | category | flops | bytes accessed | tf_op | source)
XLA Modules:
  0.0 246.1 jit_solution(7362861522683950458)
XLA Ops:
  0.6 17.5 %gather_features.1 = bf16[2,4,2,224,128]{4,3,2,1,0:T(8,128)(2,1)} custom-call(bf16[224,128]{1,0:T(8,128)(2,1)} %bitcast.40), custom_call_target="tpu_custom_call" | custom-call | tf_op jit(solution)/shard_map/gather_features/pallas_call | solution.py:215
  18.1 0.0 copy-start.1
  18.1 4.3 %fusion.81 = f32[128,896]{1,0:T(8,128)S(1)} fusion(bf16[3584,128]{1,0:T(8,128)(2,1)} %bitcast.25, bf16[3584,896]{1,0:T(8,128)(2,1)} %param.10), kind=kOutput, calls=%fused_computation.83 | convolution fusion | flops 822083584 | bytes 7798784 | tf_op jit(solution)/shard_map/dot_general | solution.py:387
  22.5 0.0 copy-done.1
  22.5 0.0 copy-start.13
  22.5 7.8 %convolution_convert_fusion.1 = bf16[128,3584]{1,0:T(8,128)(2,1)} fusion(bf16[896,3584]{1,0:T(8,128)(2,1)} %param.12, bf16[3584,128]{1,0:T(8,128)(2,1)S(1)} %bitcast.26, bf16[3584,896]{1,0:T(8,128)(2,1)} %param.11, f32[128,896]{1,0:T(8,128)S(1)} %fusion.81), kind=kOutput, calls=%fused_computation.17 | convolution fusion | flops 1645772800 | bytes 15138816 | tf_op jit(solution)/shard_map/dot_general | solution.py:390
  30.3 27.6 %sum_rows.1 = bf16[2,4,2,16,1792]{4,3,2,1,0:T(8,128)(2,1)} custom-call(bf16[4,2,16,3584]{3,2,1,0:T(8,128)(2,1)} %bitcast.28), custom_call_target="tpu_custom_call" | custom-call | tf_op jit(solution)/shard_map/sum_rows/pallas_call | solution.py:246
  58.0 0.0 copy-done.13
  58.0 0.1 reshape.39
  58.1 0.1 eq.10
  58.2 1.6 convolution_convert_fusion.2.left_ref
  59.8 0.0 copy-start
  59.9 4.5 %fusion.34 = bf16[128,2048]{1,0:T(8,128)(2,1)S(1)} fusion(bf16[1792,4096]{1,0:T(8,128)(2,1)} %param.13, bf16[256,1792]{1,0:T(8,128)(2,1)S(1)} %convolution_convert_fusion.2.left_ref), kind=kOutput, calls=%fused_computation.29 | convolution fusion | flops 939786240 | bytes 8323072 | tf_op jit(solution)/shard_map/dot_general | solution.py:419
  64.4 1.6 collective-permute-start.1
  66.0 4.4 %fusion.28 = bf16[128,2048]{1,0:T(8,128)(2,1)S(1)} fusion(bf16[1792,4096]{1,0:T(8,128)(2,1)} %param.13, bf16[256,1792]{1,0:T(8,128)(2,1)S(1)} %convolution_convert_fusion.2.left_ref), kind=kOutput, calls=%fused_computation.27 | convolution fusion | flops 939786240 | bytes 8323072 | tf_op jit(solution)/shard_map/dot_general | solution.py:419
  70.3 0.6 collective-permute-start
  70.9 0.0 copy-done
  70.9 0.8 fusion.79
  71.8 4.4 %fusion.37 = bf16[128,2048]{1,0:T(8,128)(2,1)S(1)} fusion(bf16[128,1792]{1,0:T(8,128)(2,1)S(1)} %get-tuple-element.11, bf16[1792,4096]{1,0:T(8,128)(2,1)} %param.13), kind=kOutput, calls=%fused_computation.30 | convolution fusion | flops 939786240 | bytes 8323072 | tf_op jit(solution)/shard_map/dot_general | solution.py:419
  76.2 0.0 copy-start.12
  76.2 0.0 copy-start.11
  76.2 0.0 slice-start.3
  76.2 1.6 collective-permute-start.3
  77.8 5.0 %fusion.31 = bf16[128,2048]{1,0:T(8,128)(2,1)} fusion(bf16[128,1792]{1,0:T(8,128)(2,1)S(1)} %get-tuple-element.11, bf16[1792,4096]{1,0:T(8,128)(2,1)} %param.13), kind=kOutput, calls=%fused_computation.28 | convolution fusion | flops 939786240 | bytes 8323072 | tf_op jit(solution)/shard_map/dot_general | solution.py:419
  82.8 0.6 collective-permute-start.2
  83.4 0.6 broadcast_in_dim.2.bias_ref
  84.0 0.0 collective-permute-done.1
  84.0 0.8 fusion.51
  84.8 1.1 fusion.2
  86.0 4.5 %collective-permute-done = bf16[128,2048]{1,0:T(8,128)(2,1)S(1)} collective-permute-done((bf16[128,2048]{1,0:T(8,128)(2,1)S(1)}, bf16[128,2048]{1,0:T(8,128)(2,1)S(1)}, u32[]{:S(2)}, u32[]{:S(2)}) %collective-permute-start) | collective-permute-done | bytes 524320 | tf_op jit(solution)/shard_map/ppermute | solution.py:361
  90.5 0.0 copy-done.5
  90.5 0.8 fusion.49
  91.3 0.0 copy-start.6
  91.3 2.1 fusion.25
  93.4 0.0 copy-done.6
  93.4 21.9 %shard_map.112 = (bf16[2,4,2,8,1792]{4,3,2,1,0:T(8,128)(2,1)}, bf16[8,1792]{1,0:T(8,128)(2,1)}) custom-call(bf16[2,4,2,8,1792]{4,3,2,1,0:T(8,128)(2,1)} %bitcast.37, bf16[2,4,2,8,1792]{4,3,2,1,0:T(8,128)(2,1)} %bitcast.30, f32[1,1792]{1,0:T(1,128)} %broadcast_in_dim.2.bias_ref), custom_call_target="tpu_custom_call" | custom-call | tf_op jit(solution)/shard_map/pallas_call | solution.py:264
  115.4 6.2 %turn.4 = bf16[128,2048]{1,0:T(8,128)(2,1)} custom-call(bf16[128,1792]{1,0:T(8,128)(2,1)} %bitcast.31, bf16[4096,1792]{1,0:T(8,128)(2,1)} %decoder_ref.7), custom_call_target="tpu_custom_call" | custom-call | flops 939524096 | bytes 8323072 | tf_op jit(solution)/shard_map/turn/pallas_call | solution.py:291
  121.5 0.0 collective-permute-done.3
  121.5 0.8 fusion.55
  122.3 0.8 copy-done.7
  123.1 4.2 %fusion = f32[128,1792]{1,0:T(8,128)S(1)} fusion(bf16[128,2048]{1,0:T(8,128)(2,1)S(1)} %fusion.55, bf16[4096,1792]{1,0:T(8,128)(2,1)} %decoder_ref.7), kind=kOutput, calls=%fused_computation.1 | convolution fusion | flops 939524096 | bytes 8781824 | tf_op jit(solution)/shard_map/dot_general | solution.py:435
  127.3 0.0 collective-permute-done.2
  127.3 2.0 fusion.53
  129.3 0.8 copy-done.8
  130.1 5.0 %fusion.22 = bf16[128,1792]{1,0:T(8,128)(2,1)} fusion(f32[128,1792]{1,0:T(8,128)S(1)} %fusion, bf16[128,2048]{1,0:T(8,128)(2,1)S(1)} %fusion.53, bf16[4096,1792]{1,0:T(8,128)(2,1)} %decoder_ref.7), kind=kOutput, calls=%fused_computation.25 | convolution fusion | flops 939982848 | bytes 9240576 | tf_op jit(solution)/shard_map/dot_general | solution.py:435
  135.1 22.1 %shard_map.113 = (bf16[2,4,2,8,1792]{4,3,2,1,0:T(8,128)(2,1)}, bf16[8,1792]{1,0:T(8,128)(2,1)}) custom-call(bf16[2,4,2,8,1792]{4,3,2,1,0:T(8,128)(2,1)} %bitcast.38, bf16[2,4,2,8,1792]{4,3,2,1,0:T(8,128)(2,1)} %bitcast.29, f32[1,1792]{1,0:T(1,128)} %broadcast_in_dim.2.bias_ref), custom_call_target="tpu_custom_call" | custom-call | tf_op jit(solution)/shard_map/pallas_call | solution.py:264
  157.2 6.2 %turn.5 = bf16[128,2048]{1,0:T(8,128)(2,1)} custom-call(bf16[128,1792]{1,0:T(8,128)(2,1)} %bitcast.34, bf16[4096,1792]{1,0:T(8,128)(2,1)} %decoder_ref.7), custom_call_target="tpu_custom_call" | custom-call | flops 939524096 | bytes 8323072 | tf_op jit(solution)/shard_map/turn/pallas_call | solution.py:291
  163.3 6.1 %turn.7 = bf16[128,2048]{1,0:T(8,128)(2,1)} custom-call(bf16[128,1792]{1,0:T(8,128)(2,1)} %bitcast.35, bf16[4096,1792]{1,0:T(8,128)(2,1)} %decoder_ref.7), custom_call_target="tpu_custom_call" | custom-call | flops 939524096 | bytes 8323072 | tf_op jit(solution)/shard_map/turn/pallas_call | solution.py:291
  169.5 6.1 %turn.6 = bf16[128,2048]{1,0:T(8,128)(2,1)} custom-call(bf16[128,1792]{1,0:T(8,128)(2,1)} %bitcast.32, bf16[4096,1792]{1,0:T(8,128)(2,1)} %decoder_ref.7), custom_call_target="tpu_custom_call" | custom-call | flops 939524096 | bytes 8323072 | tf_op jit(solution)/shard_map/turn/pallas_call | solution.py:291
  175.6 1.4 collective-permute-start.5
  177.0 0.6 collective-permute-start.4
  177.6 1.4 collective-permute-start.7
  179.0 0.6 collective-permute-start.6
  179.7 0.0 copy-done.9
  179.7 0.6 pad_maximum_fusion
  180.3 11.3 %convolution_convert_fusion = bf16[4096,1792]{1,0:T(8,128)(2,1)} fusion(bf16[128,2048]{1,0:T(8,128)(2,1)} %copy-done.7, bf16[128,2048]{1,0:T(8,128)(2,1)} %copy-done.8, bf16[128,2048]{1,0:T(8,128)(2,1)} %copy-done.5, bf16[128,2048]{1,0:T(8,128)(2,1)} %copy-done.6, bf16[128,1792]{1,0:T(8,128)(2,1)} %bitcast.36, bf16[128,1792]{1,0:T(8,128)(2,1)} %bitcast.33), kind=kOutput, calls=%fused_computation | convolution fusion | flops 3775660032 | bytes 17694720 | tf_op jit(solution)/shard_map/dot_general | solution.py:470
  191.6 21.6 %collective-permute-done.7 = bf16[128,2048]{1,0:T(8,128)(2,1)} collective-permute-done((bf16[128,2048]{1,0:T(8,128)(2,1)}, bf16[128,2048]{1,0:T(8,128)(2,1)}, u32[]{:S(2)}, u32[]{:S(2)}) %collective-permute-start.7) | collective-permute-done | bytes 524320 | tf_op jit(solution)/shard_map/ppermute | solution.py:361
  213.2 10.6 %collective-permute-done.6 = bf16[128,2048]{1,0:T(8,128)(2,1)} collective-permute-done((bf16[128,2048]{1,0:T(8,128)(2,1)}, bf16[128,2048]{1,0:T(8,128)(2,1)}, u32[]{:S(2)}, u32[]{:S(2)}) %collective-permute-start.6) | collective-permute-done | bytes 524320 | tf_op jit(solution)/shard_map/ppermute | solution.py:361
  223.8 3.8 %multiply_convert_fusion = (bf16[128,2048]{1,0:T(8,128)(2,1)}, bf16[128,2048]{1,0:T(8,128)(2,1)}) fusion(bf16[128,2048]{1,0:T(8,128)(2,1)} %collective-permute-done.7, bf16[128,2048]{1,0:T(8,128)(2,1)} %turn.7, bf16[128,2048]{1,0:T(8,128)(2,1)} %collective-permute-done.2, bf16[128,2048]{1,0:T(8,128)(2,1)} %fusion.31, f32[2048]{0:T(1024)S(1)} %get-tuple-element.19, ...), kind=kLoop, calls=%fused_computation.48 | loop fusion | flops 7340032 | bytes 5251072 | tf_op jit(solution)/shard_map/convert_element_type | solution.py:468
  227.7 7.7 %shard_map.114.refs_2_ = bf16[1792,4096]{1,0:T(8,128)(2,1)} custom-call(bf16[256,1792]{1,0:T(8,128)(2,1)} %copy-done, bf16[128,2048]{1,0:T(8,128)(2,1)} %get-tuple-element.22.refs_0_, bf16[128,2048]{1,0:T(8,128)(2,1)} %get-tuple-element.21.refs_1_), custom_call_target="tpu_custom_call" | custom-call | flops 1879048192 | bytes 9306112 | tf_op jit(solution)/shard_map/pallas_call | solution.py:339
  235.3 0.0 collective-permute-done.5
  235.3 0.0 collective-permute-done.4
  235.4 3.2 %multiply_convert_fusion.2 = (bf16[128,2048]{1,0:T(8,128)(2,1)}, bf16[128,2048]{1,0:T(8,128)(2,1)}) fusion(bf16[128,2048]{1,0:T(8,128)(2,1)} %collective-permute-done.5, bf16[128,2048]{1,0:T(8,128)(2,1)S(1)} %copy-done.3, bf16[128,2048]{1,0:T(8,128)(2,1)S(1)} %collective-permute-done.3, bf16[128,2048]{1,0:T(8,128)(2,1)S(1)} %fusion.37, ...), kind=kLoop, calls=%fused_computation.50 | loop fusion | flops 7340032 | bytes 5251072 | tf_op jit(solution)/shard_map/convert_element_type | solution.py:468
  238.5 7.6 %shard_map.115 = bf16[1792,4096]{1,0:T(8,128)(2,1)} custom-call(bf16[256,1792]{1,0:T(8,128)(2,1)} %copy-done, bf16[128,2048]{1,0:T(8,128)(2,1)} %get-tuple-element.24.refs_0_, bf16[128,2048]{1,0:T(8,128)(2,1)} %get-tuple-element.23.refs_1_, bf16[1792,4096]{1,0:T(8,128)(2,1)} %shard_map.114.refs_2_), custom_call_target="tpu_custom_call", output_to_operand_aliasing={{}: (3, {})} | custom-call | flops 1879048192 | bytes 9306112 | tf_op jit(solution)/shard_map/pallas_call | solution.py:339
  (24 shorter events, 0.0 us)
Async XLA Ops:
  18.1 4.4 %copy-start.1 = (bf16[2,4,2,224,128]{4,3,2,1,0:T(8,128)(2,1)S(1)}, bf16[2,4,2,224,128]{4,3,2,1,0:T(8,128)(2,1)}, u32[]{:S(2)}) copy-start(bf16[2,4,2,224,128]{4,3,2,1,0:T(8,128)(2,1)} %gather_features.1) | copy-start | bytes 2752516
  22.5 35.5 %copy-start.13 = (s32[256]{0:T(256)S(1)}, s32[256]{0:T(256)}, u32[]{:S(2)}) copy-start(s32[256]{0:T(256)} %param.17) | copy-start | bytes 3076
  59.8 11.1 %copy-start = (bf16[256,1792]{1,0:T(8,128)(2,1)}, bf16[256,1792]{1,0:T(8,128)(2,1)S(1)}, u32[]{:S(2)}) copy-start(bf16[256,1792]{1,0:T(8,128)(2,1)S(1)} %convolution_convert_fusion.2.left_ref) | copy-start | bytes 2752516
  64.4 19.6 %collective-permute-start.1 = (bf16[128,2048]{1,0:T(8,128)(2,1)S(1)}, bf16[128,2048]{1,0:T(8,128)(2,1)S(1)}, u32[]{:S(2)}, u32[]{:S(2)}) collective-permute-start(bf16[128,2048]{1,0:T(8,128)(2,1)S(1)} %fusion.34), channel_id=1, source_target_pairs={{0,8},{8,0},{1,9},{9,1},{2,10},{10,2},{3,11},{11,3},{4,12},{12,4},... | collective-permute-start | bytes 1572872 | tf_op jit(solution)/shard_map/ppermute | solution.py:361
  66.0 18.8 %slice-start = ((s8[14680064]{0:T(1024)(128)(4,1)}), s8[4194304]{0:T(1024)(128)(4,1)S(1)}, s32[]{:S(2)}) async-start(s8[14680064]{0:T(1024)(128)(4,1)} %bitcast.23), calls=%async_computation | async-start | bytes 8388608
  66.0 18.8 %slice-start.1 = ((s8[14680064]{0:T(1024)(128)(4,1)}), s8[4194304]{0:T(1024)(128)(4,1)S(1)}, s32[]{:S(2)}) async-start(s8[14680064]{0:T(1024)(128)(4,1)} %bitcast.23), calls=%async_computation.1 | async-start | bytes 8388608
  70.3 20.2 %collective-permute-start = (bf16[128,2048]{1,0:T(8,128)(2,1)S(1)}, bf16[128,2048]{1,0:T(8,128)(2,1)S(1)}, u32[]{:S(2)}, u32[]{:S(2)}) collective-permute-start(bf16[128,2048]{1,0:T(8,128)(2,1)S(1)} %fusion.28), channel_id=1, source_target_pairs={{0,8},{8,0},{1,9},{9,1},{2,10},{10,2},{3,11},{11,3},{4,12},{12,4},... | collective-permute-start | bytes 1572872 | tf_op jit(solution)/shard_map/ppermute | solution.py:361
  71.8 11.0 %copy-start.4 = (bf16[128,1792]{1,0:T(8,128)(2,1)}, bf16[128,1792]{1,0:T(8,128)(2,1)S(1)}, u32[]{:S(2)}) copy-start(bf16[128,1792]{1,0:T(8,128)(2,1)S(1)} %get-tuple-element.11) | copy-start | bytes 1376260
  71.8 13.0 %slice-start.2 = ((s8[14680064]{0:T(1024)(128)(4,1)}), s8[4194304]{0:T(1024)(128)(4,1)S(1)}, s32[]{:S(2)}) async-start(s8[14680064]{0:T(1024)(128)(4,1)} %bitcast.23), calls=%async_computation.2 | async-start | bytes 8388608
  76.2 7.2 %copy-start.12 = (f32[1792]{0:T(1024)S(1)}, f32[1792]{0:T(1024)}, u32[]{:S(2)}) copy-start(f32[1792]{0:T(1024)} %param.16) | copy-start | bytes 21508
  76.2 7.8 %copy-start.11 = (f32[4096]{0:T(1024)S(1)}, f32[4096]{0:T(1024)}, u32[]{:S(2)}) copy-start(f32[4096]{0:T(1024)} %param.15) | copy-start | bytes 49156
  76.2 8.6 %slice-start.3 = ((s8[14680064]{0:T(1024)(128)(4,1)}), s8[2097152]{0:T(1024)(128)(4,1)S(1)}, s32[]{:S(2)}) async-start(s8[14680064]{0:T(1024)(128)(4,1)} %bitcast.23), calls=%async_computation.3 | async-start | bytes 4194304
  76.2 45.3 %collective-permute-start.3 = (bf16[128,2048]{1,0:T(8,128)(2,1)S(1)}, bf16[128,2048]{1,0:T(8,128)(2,1)S(1)}, u32[]{:S(2)}, u32[]{:S(2)}) collective-permute-start(bf16[128,2048]{1,0:T(8,128)(2,1)S(1)} %fusion.37), channel_id=1, source_target_pairs={{0,8},{8,0},{1,9},{9,1},{2,10},{10,2},{3,11},{11,3},{4,12},{12,4},... | collective-permute-start | bytes 1572872 | tf_op jit(solution)/shard_map/ppermute | solution.py:361
  82.8 44.6 %collective-permute-start.2 = (bf16[128,2048]{1,0:T(8,128)(2,1)}, bf16[128,2048]{1,0:T(8,128)(2,1)}, u32[]{:S(2)}, u32[]{:S(2)}) collective-permute-start(bf16[128,2048]{1,0:T(8,128)(2,1)} %fusion.31), channel_id=1, source_target_pairs={{0,8},{8,0},{1,9},{9,1},{2,10},{10,2},{3,11},{11,3},{4,12},{12,4},... | collective-permute-start | bytes 1572872 | tf_op jit(solution)/shard_map/ppermute | solution.py:361
  84.8 5.7 %copy-start.5 = (bf16[128,2048]{1,0:T(8,128)(2,1)}, bf16[128,2048]{1,0:T(8,128)(2,1)S(1)}, u32[]{:S(2)}) copy-start(bf16[128,2048]{1,0:T(8,128)(2,1)S(1)} %fusion.51) | copy-start | bytes 1572868
  91.3 2.1 copy-start.6
  122.3 0.8 copy-start.7
  129.3 0.8 copy-start.8
  169.5 10.2 %copy-start.9 = (bf16[8,1792]{1,0:T(8,128)(2,1)S(1)}, bf16[8,1792]{1,0:T(8,128)(2,1)}, u32[]{:S(2)}) copy-start(bf16[8,1792]{1,0:T(8,128)(2,1)} %get-tuple-element.10) | copy-start | bytes 86020
  169.5 10.2 %copy-start.10 = (bf16[8,1792]{1,0:T(8,128)(2,1)S(1)}, bf16[8,1792]{1,0:T(8,128)(2,1)}, u32[]{:S(2)}) copy-start(bf16[8,1792]{1,0:T(8,128)(2,1)} %get-tuple-element.15) | copy-start | bytes 86020
  175.6 59.7 %collective-permute-start.5 = (bf16[128,2048]{1,0:T(8,128)(2,1)}, bf16[128,2048]{1,0:T(8,128)(2,1)}, u32[]{:S(2)}, u32[]{:S(2)}) collective-permute-start(bf16[128,2048]{1,0:T(8,128)(2,1)} %turn.5), channel_id=1, source_target_pairs={{0,8},{8,0},{1,9},{9,1},{2,10},{10,2},{3,11},{11,3},{4,12},{12,4},... | collective-permute-start | bytes 1572872 | tf_op jit(solution)/shard_map/ppermute | solution.py:361
  177.0 58.3 %collective-permute-start.4 = (bf16[128,2048]{1,0:T(8,128)(2,1)}, bf16[128,2048]{1,0:T(8,128)(2,1)}, u32[]{:S(2)}, u32[]{:S(2)}) collective-permute-start(bf16[128,2048]{1,0:T(8,128)(2,1)} %turn.4), channel_id=1, source_target_pairs={{0,8},{8,0},{1,9},{9,1},{2,10},{10,2},{3,11},{11,3},{4,12},{12,4},... | collective-permute-start | bytes 1572872 | tf_op jit(solution)/shard_map/ppermute | solution.py:361
  177.6 35.6 %collective-permute-start.7 = (bf16[128,2048]{1,0:T(8,128)(2,1)}, bf16[128,2048]{1,0:T(8,128)(2,1)}, u32[]{:S(2)}, u32[]{:S(2)}) collective-permute-start(bf16[128,2048]{1,0:T(8,128)(2,1)} %turn.7), channel_id=1, source_target_pairs={{0,8},{8,0},{1,9},{9,1},{2,10},{10,2},{3,11},{11,3},{4,12},{12,4},... | collective-permute-start | bytes 1572872 | tf_op jit(solution)/shard_map/ppermute | solution.py:361
  179.0 44.8 %collective-permute-start.6 = (bf16[128,2048]{1,0:T(8,128)(2,1)}, bf16[128,2048]{1,0:T(8,128)(2,1)}, u32[]{:S(2)}, u32[]{:S(2)}) collective-permute-start(bf16[128,2048]{1,0:T(8,128)(2,1)} %turn.6), channel_id=1, source_target_pairs={{0,8},{8,0},{1,9},{9,1},{2,10},{10,2},{3,11},{11,3},{4,12},{12,4},... | collective-permute-start | bytes 1572872 | tf_op jit(solution)/shard_map/ppermute | solution.py:361
  227.7 7.7 %copy-start.2 = (bf16[128,2048]{1,0:T(8,128)(2,1)S(1)}, bf16[128,2048]{1,0:T(8,128)(2,1)}, u32[]{:S(2)}) copy-start(bf16[128,2048]{1,0:T(8,128)(2,1)} %turn.4) | copy-start | bytes 1572868
  227.7 7.7 %copy-start.3 = (bf16[128,2048]{1,0:T(8,128)(2,1)S(1)}, bf16[128,2048]{1,0:T(8,128)(2,1)}, u32[]{:S(2)}) copy-start(bf16[128,2048]{1,0:T(8,128)(2,1)} %turn.5) | copy-start | bytes 1572868
